TPU v7x, 32 devices: a whole 2x2x4 slice. The times are simulated.
32 devices in a mesh: rep: 2 (over x), shard: 16 (over z, y, core).
Axes of the slice: x: 2, y: 2, z: 4, core: 2. Of those that a mesh axis runs over, the one named last changes fastest.
Arguments:
- hidden: bfloat16 [12288, 64], P(('rep', 'shard')), may hold values from -6 to 6
- grad_out: bfloat16 [12288, 4096], P(('rep', 'shard')), may hold values from -6 to 6
- weight_band: bfloat16 [64, 4096], P('shard'), may hold values from -0.09375 to 0.09375
- error_feedback: float32 [2, 64, 4096], P('rep', 'shard'), may hold values from -4.2426405 to 4.2426405
- q_start: float32 [4096, 32], replicated, may hold values from -6 to 6
Outputs:
- update: float32 [64, 4096], P('shard')
- error_next: float32 [2, 64, 4096], P('rep', 'shard')
- q_next: float32 [4096, 32], replicated
- d_hidden: bfloat16 [12288, 64], P(('rep', 'shard'))
All inputs are finite; a program needn't handle non-finite values.
Results may differ from a plain program's by a relative error of at most 0.0004.
Values may be sent and summed in bfloat16 or wider, within the bound.
A program may use at most 64 MiB of HBM per device.

v0:
```python
import math
import jax
import jax.numpy as jnp
from jax import lax
from jax.sharding import PartitionSpec as P

POWER = 2


def orthonormal(matrix):
    gram_matrix = jnp.dot(matrix.T, matrix, precision=lax.Precision.HIGHEST)
    factor_low = jnp.linalg.cholesky(gram_matrix)
    return lax.linalg.triangular_solve(
        factor_low, matrix, left_side=False, lower=True, transpose_a=True
    )


def orth_rows(p_local):
    all_rows = lax.all_gather(p_local, "shard", axis=0, tiled=True)
    gram_matrix = jnp.dot(all_rows.T, all_rows, precision=lax.Precision.HIGHEST)
    factor_low = jnp.linalg.cholesky(gram_matrix)
    return lax.linalg.triangular_solve(
        factor_low, p_local, left_side=False, lower=True, transpose_a=True
    )


def body(hidden, grad_out, weight_band, error_feedback, q_start):
    n_rep = lax.axis_size("rep")
    n_shard = lax.axis_size("shard")
    token_rows = hidden.shape[0]
    grad_scale = 1.0 / math.sqrt(token_rows * n_shard * n_rep)
    d_hidden = lax.dot_general(
        grad_out,
        lax.all_gather(weight_band, "shard", axis=0, tiled=True),
        (((1,), (1,)), ((), ())),
        preferred_element_type=jnp.float32,
    ).astype(jnp.bfloat16)
    grad_rows = lax.psum_scatter(
        lax.dot_general(
            hidden, grad_out, (((0,), (0,)), ((), ())), preferred_element_type=jnp.float32
        )
        * grad_scale,
        "shard",
        scatter_dimension=0,
        tiled=True,
    )
    own_rows = grad_rows + error_feedback[0]
    q_factor = q_start
    p_factor = None
    for round_index in range(POWER):
        q_hat = orthonormal(q_factor)
        p_local = jnp.dot(own_rows, q_hat, precision=lax.Precision.HIGHEST)
        p_factor = orth_rows(lax.psum(p_local, "rep"))
        q_term = lax.dot_general(
            own_rows, p_factor, (((0,), (0,)), ((), ())), precision=lax.Precision.HIGHEST
        )
        q_factor = lax.psum(q_term, ("rep", "shard"))
    update = jnp.dot(p_factor, q_factor.T, precision=lax.Precision.HIGHEST)
    error_next = own_rows - update / n_rep
    return (update, error_next[None], q_factor, d_hidden)


def solution(mesh):
    return jax.shard_map(
        body,
        mesh=mesh,
        in_specs=(
            P(("rep", "shard"), None),
            P(("rep", "shard"), None),
            P("shard", None),
            P("rep", "shard", None),
            P(),
        ),
        out_specs=(P("shard", None), P("rep", "shard", None), P(), P(("rep", "shard"), None)),
        check_vma=False,
    )
```

profile of v0, /device:TPU:0, one launch (start us, length us, event | category | flops | bytes accessed | tf_op | source)
XLA Modules:
  0.0 451.4 jit_solution(12840853244050156011)
XLA Ops:
  7.2 1.8 copy-done
  9.1 2.5 convolution_multiply_fusion
  11.6 1.8 fusion.18
  13.5 2.9 cholesky.74
  17.8 2.4 custom-call.10
  21.5 2.5 convolution_bitcast_fusion.1
  23.9 84.3 %all-reduce.9.cloned.1.call-done = f32[64,4096]{1,0:T(8,128)} async-done(((f32[64,4096]{1,0:T(8,128)}), f32[64,4096]{1,0:T(8,128)}) %all-reduce.9.cloned.1.call-update) | async-done | bytes 1048592
  110.7 4.9 %psum.28 = f32[4,32]{1,0:T(4,128)S(1)} all-reduce(f32[4,32]{1,0:T(4,128)S(1)} %fusion.19), channel_id=1, replica_groups=mesh['rep'=2,'shard'=16] {'rep'}, use_global_device_ids=true, to_apply=%region_3.6 | all-reduce | flops 128 | bytes 1024 | tf_op jit(solution)/shard_map/psum | solution.py:53
  115.7 19.5 %all-gather = f32[16,4,32]{2,1,0:T(4,128)S(1)} all-gather(f32[1,4,32]{2,1,0:T(4,128)S(1)} %bitcast.83), channel_id=1, replica_groups=mesh['rep'=2,'shard'=16] {'shard'}, dimensions={0}, use_global_device_ids=true | all-gather | bytes 8704 | tf_op jit(solution)/shard_map/all_gather | solution.py:19
  135.5 2.9 cholesky.85
  139.7 2.5 custom-call.11
  143.9 20.5 %all-gather.2 = bf16[16,4,4096]{2,1,0:T(4,128)(2,1)} all-gather(bf16[1,4,4096]{2,1,0:T(4,128)(2,1)S(1)} %bitcast.82), channel_id=1, replica_groups=mesh['rep'=2,'shard'=16] {'shard'}, dimensions={0}, use_global_device_ids=true | all-gather | bytes 557056 | tf_op jit(solution)/shard_map/all_gather | solution.py:34
  164.4 2.0 reshape.34
  166.3 104.4 %all-reduce.5.cloned.1.call-done = f32[4096,32]{0,1:T(8,128)} async-done(((f32[4096,32]{0,1:T(8,128)}), f32[4096,32]{0,1:T(8,128)}) %all-reduce.5.cloned.1.call-update) | async-done | bytes 524304 | tf_op jit(solution)/shard_map/psum | solution.py:57
  270.7 1.8 fusion.22
  272.5 2.9 cholesky.96
  276.8 2.4 custom-call.12
  281.4 4.9 %psum.30 = f32[4,32]{1,0:T(4,128)S(1)} all-reduce(f32[4,32]{1,0:T(4,128)S(1)} %fusion.23), channel_id=1, replica_groups=mesh['rep'=2,'shard'=16] {'rep'}, use_global_device_ids=true, to_apply=%region_5.9 | all-reduce | flops 128 | bytes 1024 | tf_op jit(solution)/shard_map/psum | solution.py:53
  286.4 20.4 %all-gather.1 = f32[16,4,32]{2,1,0:T(4,128)S(1)} all-gather(f32[1,4,32]{2,1,0:T(4,128)S(1)} %bitcast.84), channel_id=1, replica_groups=mesh['rep'=2,'shard'=16] {'shard'}, dimensions={0}, use_global_device_ids=true | all-gather | bytes 8704 | tf_op jit(solution)/shard_map/all_gather | solution.py:19
  307.0 2.9 cholesky.107
  311.3 2.5 custom-call.13
  315.3 2.7 convolution_convert_fusion
  318.1 122.9 %all-reduce.7.cloned.1.call-done = f32[4096,32]{0,1:T(8,128)} async-done(((f32[4096,32]{0,1:T(8,128)}), f32[4096,32]{0,1:T(8,128)}) %all-reduce.7.cloned.1.call-update) | async-done | bytes 524304 | tf_op jit(solution)/shard_map/psum | solution.py:57
  443.0 1.9 copy.20
  (48 shorter events, 16.7 us)
Async XLA Ops:
  7.2 1.9 copy-start
  7.2 13.0 %copy-start.4 = (u32[32]{0:T(128)S(1)}, u32[32]{0:T(128)}, u32[]{:S(2)}) copy-start(u32[32]{0:T(128)} %constant.41) | copy-start | bytes 388
  7.2 101.1 %copy-start.2 = (f32[1,4,4096]{2,1,0:T(4,128)S(1)}, f32[1,4,4096]{2,1,0:T(4,128)}, u32[]{:S(2)}) copy-start(f32[1,4,4096]{2,1,0:T(4,128)} %param.13) | copy-start | bytes 196612
  7.2 101.1 %all-reduce.9.cloned.1.call-start = ((), (), s32[]{:S(2)}) async-start(), calls=%async_computation.2 | async-start | bytes 2097152
  11.6 132.3 %copy-start.3 = (bf16[4,4096]{1,0:T(4,128)(2,1)S(1)}, bf16[4,4096]{1,0:T(4,128)(2,1)}, u32[]{:S(2)}) copy-start(bf16[4,4096]{1,0:T(4,128)(2,1)} %param.12) | copy-start | bytes 98308
  11.6 259.1 %all-reduce.5.cloned.1.call-start = ((), (), s32[]{:S(2)}) async-start(), calls=%async_computation | async-start | bytes 1048576 | tf_op jit(solution)/shard_map/psum | solution.py:57
  143.8 297.2 %all-reduce.7.cloned.1.call-start = ((), (), s32[]{:S(2)}) async-start(), calls=%async_computation.1 | async-start | bytes 1048576 | tf_op jit(solution)/shard_map/psum | solution.py:57
  442.4 2.5 copy-start.1
Sparse Core Ops, SparseCore 0:
  11.7 96.4 all-reduce.8
  143.9 126.7 all-reduce.4
  315.5 125.4 all-reduce.6
where the time goes:
time: 452 us; the launch traced here: 451 us
  waiting for transfers between devices  312 us (69%)
  blocking collectives  70.2 us (16%)
  other arithmetic  28.4 us (6%)
  matrix products  19.9 us (4%)
  between operations  14.6 us (3%)
  local copies, waits for them, and re-layouts  6.59 us (1%)
    psum x2, waiting for transfers between devices, body(): q_factor = lax.psum(q_term, ('rep', 'shard'))  227 us
    unnamed x4, waiting for transfers between devices  84.4 us
    all_gather x2, blocking collectives, orth_rows(): all_rows = lax.all_gather(p_local, 'shard', axis=0, tiled=True)  39.9 us
    all_gather x1, blocking collectives, body(): lax.all_gather(weight_band, 'shard', axis=0, tiled=True)  20.5 us
    psum x2, blocking collectives, body(): p_factor = orth_rows(lax.psum(p_local, 'rep'))  9.85 us
  transfers between devices with their start and end apart: 3, of which 3 were waited for; matrix products, arithmetic and copies ran while one was open for 4% of the time, Pallas kernels for 0%

commit v1 on v0

--- a/solution.py
+++ b/solution.py
@@ -1,3 +1,4 @@
+import functools
 import math
 import jax
 import jax.numpy as jnp
@@ -5,6 +6,13 @@
 from jax.sharding import PartitionSpec as P
 
 POWER = 2
+
+
+def watch_sectors(panel, axis_name):
+    return jnp.sum(lax.all_gather(panel, axis_name), 0)
+
+
+build_digits = functools.partial(watch_sectors, axis_name=("rep", "shard"))
 
 
 def orthonormal(matrix):
@@ -54,7 +62,7 @@
         q_term = lax.dot_general(
             own_rows, p_factor, (((0,), (0,)), ((), ())), precision=lax.Precision.HIGHEST
         )
-        q_factor = lax.psum(q_term, ("rep", "shard"))
+        q_factor = build_digits(q_term)
     update = jnp.dot(p_factor, q_factor.T, precision=lax.Precision.HIGHEST)
     error_next = own_rows - update / n_rep
     return (update, error_next[None], q_factor, d_hidden)

time: 452 us -> 475 us (1.051)
  local copies, waits for them, and re-layouts: 6.59 us -> 40.1 us
  waiting for transfers between devices: 312 us -> 282 us
  other arithmetic: 28.4 us -> 47 us
    psum x2 -> x0, waiting for transfers between devices: 227 us -> none  [body(): q_factor = lax.psum(q_term, ('rep', 'shard'))]
    all_gather x0 -> x2, waiting for transfers between devices: none -> 197 us  [watch_sectors(): return jnp.sum(lax.all_gather(panel, axis_name), 0)]
    unnamed x13 -> x16, local copies, waits for them, and re-layouts: 6.29 us -> 39.8 us
    reduce_sum x0 -> x2, other arithmetic: none -> 18.6 us  [watch_sectors(): return jnp.sum(lax.all_gather(panel, axis_name), 0)]
  transfers between devices with their start and end apart: 3 -> 3, of which waited for: 3 -> 3; matrix products, arithmetic and copies ran while one was open for 4% -> 3% of each run, Pallas kernels for 0% -> 0%
where the time goes in v1:
time: 475 us
  waiting for transfers between devices  282 us (59%)
  blocking collectives  70.8 us (15%)
  other arithmetic  47 us (10%)
  local copies, waits for them, and re-layouts  40.1 us (8%)
  matrix products  20.1 us (4%)
  between operations  14.6 us (3%)
    all_gather x2, waiting for transfers between devices, watch_sectors(): return jnp.sum(lax.all_gather(panel, axis_name), 0)  197 us
    unnamed x4, waiting for transfers between devices  84.3 us
    unnamed x16, local copies, waits for them, and re-layouts  39.8 us
    all_gather x2, blocking collectives, orth_rows(): all_rows = lax.all_gather(p_local, 'shard', axis=0, tiled=True)  39.2 us
    all_gather x1, blocking collectives, body(): lax.all_gather(weight_band, 'shard', axis=0, tiled=True)  21.8 us
    reduce_sum x2, other arithmetic, watch_sectors(): return jnp.sum(lax.all_gather(panel, axis_name), 0)  18.6 us
    psum x2, blocking collectives, body(): p_factor = orth_rows(lax.psum(p_local, 'rep'))  9.85 us
  transfers between devices with their start and end apart: 3, of which 3 were waited for; matrix products, arithmetic and copies ran while one was open for 3% of the time, Pallas kernels for 0%

profile of v1, /device:TPU:0, one launch (start us, length us, event | category | flops | bytes accessed | tf_op | source)
XLA Modules:
  0.0 474.6 jit_solution(15815772653932079007)
XLA Ops:
  9.1 2.5 convolution_multiply_fusion
  13.6 2.9 cholesky.74
  17.8 2.4 custom-call.10
  21.5 2.5 convolution_bitcast_fusion.1
  24.0 84.2 %all-reduce.3.cloned.1.call-done = f32[64,4096]{1,0:T(8,128)} async-done(((f32[64,4096]{1,0:T(8,128)}), f32[64,4096]{1,0:T(8,128)}) %all-reduce.3.cloned.1.call-update) | async-done | bytes 1048592
  110.7 4.9 %psum.14 = f32[4,32]{1,0:T(4,128)S(1)} all-reduce(f32[4,32]{1,0:T(4,128)S(1)} %fusion.19), channel_id=1, replica_groups=mesh['rep'=2,'shard'=16] {'rep'}, use_global_device_ids=true, to_apply=%region_3.6 | all-reduce | flops 128 | bytes 1024 | tf_op jit(solution)/shard_map/psum | solution.py:61
  115.6 19.5 %all-gather.2 = f32[16,4,32]{2,1,0:T(4,128)S(1)} all-gather(f32[1,4,32]{2,1,0:T(4,128)S(1)} %bitcast.95), channel_id=1, replica_groups=mesh['rep'=2,'shard'=16] {'shard'}, dimensions={0}, use_global_device_ids=true | all-gather | bytes 8704 | tf_op jit(solution)/shard_map/all_gather | solution.py:27
  135.4 2.9 cholesky.85
  139.7 2.4 custom-call.11
  144.0 111.4 %all-gather.8.cloned.1.call-done = f32[131072,32]{0,1:T(8,128)} async-done(((f32[4096,32]{0,1:T(8,128)}), f32[131072,32]{0,1:T(8,128)}) %all-gather.8.cloned.1.call-update) | async-done | bytes 16777232 | tf_op jit(solution)/shard_map/all_gather | solution.py:12
  255.4 17.7 %copy.17 = f32[4,8,32,4096]{3,2,1,0:T(8,128)} copy(f32[4,8,32,4096]{3,1,2,0:T(8,128)} %bitcast.91) | data formatting | bytes 33554432
  273.1 9.2 %bitcast_reduce_fusion.1 = f32[4096,32]{0,1:T(8,128)} fusion(f32[4,8,32,4096]{3,2,1,0:T(8,128)} %copy.17), kind=kLoop, calls=%fused_computation.1 | loop fusion | flops 4063232 | bytes 17301504 | tf_op jit(solution)/shard_map/reduce_sum | solution.py:12
  284.2 2.9 cholesky.96
  288.5 2.4 custom-call.12
  293.1 4.9 %psum.15 = f32[4,32]{1,0:T(4,128)S(1)} all-reduce(f32[4,32]{1,0:T(4,128)S(1)} %fusion.23), channel_id=1, replica_groups=mesh['rep'=2,'shard'=16] {'rep'}, use_global_device_ids=true, to_apply=%region_5.9 | all-reduce | flops 128 | bytes 1024 | tf_op jit(solution)/shard_map/psum | solution.py:61
  298.1 19.7 %all-gather.3 = f32[16,4,32]{2,1,0:T(4,128)S(1)} all-gather(f32[1,4,32]{2,1,0:T(4,128)S(1)} %bitcast.96), channel_id=1, replica_groups=mesh['rep'=2,'shard'=16] {'shard'}, dimensions={0}, use_global_device_ids=true | all-gather | bytes 8704 | tf_op jit(solution)/shard_map/all_gather | solution.py:27
  318.0 2.9 cholesky.107
  322.3 2.4 custom-call.13
  326.3 21.8 %all-gather.4 = bf16[16,4,4096]{2,1,0:T(4,128)(2,1)} all-gather(bf16[1,4,4096]{2,1,0:T(4,128)(2,1)S(1)} %bitcast.94), channel_id=1, replica_groups=mesh['rep'=2,'shard'=16] {'shard'}, dimensions={0}, use_global_device_ids=true | all-gather | bytes 557056 | tf_op jit(solution)/shard_map/all_gather | solution.py:42
  348.1 2.0 reshape.36
  350.1 2.8 convolution_convert_fusion
  352.9 86.0 %all-gather.10.cloned.1.call-done = f32[131072,32]{0,1:T(8,128)} async-done(((f32[4096,32]{0,1:T(8,128)}), f32[131072,32]{0,1:T(8,128)}) %all-gather.10.cloned.1.call-update) | async-done | bytes 16777232 | tf_op jit(solution)/shard_map/all_gather | solution.py:12
  438.9 17.7 %copy.18 = f32[4,8,32,4096]{3,2,1,0:T(8,128)} copy(f32[4,8,32,4096]{3,1,2,0:T(8,128)} %bitcast.90) | data formatting | bytes 33554432
  456.6 9.4 %bitcast_reduce_fusion = f32[4096,32]{0,1:T(8,128)} fusion(f32[4,8,32,4096]{3,2,1,0:T(8,128)} %copy.18), kind=kLoop, calls=%fused_computation | loop fusion | flops 4063232 | bytes 17301504 | tf_op jit(solution)/shard_map/reduce_sum | solution.py:12
  (53 shorter events, 22.4 us)
Async XLA Ops:
  7.2 1.9 copy-start
  7.2 13.1 %copy-start.5 = (u32[32]{0:T(128)S(1)}, u32[32]{0:T(128)}, u32[]{:S(2)}) copy-start(u32[32]{0:T(128)} %constant.43) | copy-start | bytes 388
  7.2 101.0 %copy-start.3 = (f32[1,4,4096]{2,1,0:T(4,128)S(1)}, f32[1,4,4096]{2,1,0:T(4,128)}, u32[]{:S(2)}) copy-start(f32[1,4,4096]{2,1,0:T(4,128)} %param.13) | copy-start | bytes 196612
  7.2 101.0 %all-reduce.3.cloned.1.call-start = ((), (), s32[]{:S(2)}) async-start(), calls=%async_computation.2 | async-start | bytes 2097152
  11.6 243.8 %all-gather.8.cloned.1.call-start = ((), (), s32[]{:S(2)}) async-start(), calls=%async_computation | async-start | bytes 17301504 | tf_op jit(solution)/shard_map/all_gather | solution.py:12
  143.7 295.1 %all-gather.10.cloned.1.call-start = ((), (), s32[]{:S(2)}) async-start(), calls=%async_computation.1 | async-start | bytes 17301504 | tf_op jit(solution)/shard_map/all_gather | solution.py:12
  282.3 44.0 %copy-start.4 = (bf16[4,4096]{1,0:T(4,128)(2,1)S(1)}, bf16[4,4096]{1,0:T(4,128)(2,1)}, u32[]{:S(2)}) copy-start(bf16[4,4096]{1,0:T(4,128)(2,1)} %param.12) | copy-start | bytes 98308
  456.6 11.5 %copy-start.1 = (bf16[384,4096]{1,0:T(8,128)(2,1)S(1)}, bf16[384,4096]{1,0:T(8,128)(2,1)}, u32[]{:S(2)}) copy-start(bf16[384,4096]{1,0:T(8,128)(2,1)} %param.11) | copy-start | bytes 9437188
  467.4 0.7 copy-start.2
Sparse Core Ops, SparseCore 0:
  11.7 96.4 all-reduce.2
  143.9 111.5 all-gather.7
  326.4 112.4 all-gather.9
